TPU v7x, 32 devices: a whole 2x2x4 slice. The times are simulated.
32 devices in a mesh: rep: 2 (over y), tp: 4 (over z), ep: 4 (over x, core).
Axes of the slice: x: 2, y: 2, z: 4, core: 2. Of those that a mesh axis runs over, the one named last changes fastest.
Arguments:
- tokens: bfloat16 [768, 3072], P(('rep', 'ep'), 'tp'), parts along dimension 0, may hold values from -6 to 6
- routing: int32 [768, 2], P(('rep', 'ep')), parts along dimension 0, may hold values from 0 to 3, all different within a row; in each aligned block of 96 rows (0 to 95, 96 to 191, ...) at most 54 rows name the same one
- route_gates: float32 [768, 2], P(('rep', 'ep')), parts along dimension 0, may hold values from 0.2 to 1
- expert_gate: bfloat16 [4, 3072, 8192], P('ep', None, 'tp'), may hold values from -0.109375 to 0.109375
- expert_up: bfloat16 [4, 3072, 8192], P('ep', None, 'tp'), may hold values from -0.109375 to 0.109375
- expert_down: bfloat16 [4, 8192, 3072], P('ep', 'tp'), may hold values from -0.0625 to 0.0625
Outputs:
- mixture: bfloat16 [768, 3072], P(('rep', 'ep'), 'tp'), parts along dimension 0
There are 2 independent parts, one for each index of `rep`. A program takes and returns all parts, laid end to end along the dimension named above; an argument that names none is the same for every part. Nothing has to cross between parts.
Inputs may be any that keep to these rules, and one draw needn't show every extreme that they name: `routing`: each token names two different experts. In each aligned block of 96 tokens (the rows of one index of ep) no expert is named by more than 54 tokens, a bound that some block reaches.
All inputs are finite; a program needn't handle non-finite values.
Results may differ from a plain program's by a relative error of at most 0.0085.
Values may be sent and summed in bfloat16 or wider, within the bound.
A program may use at most 128 MiB of HBM per device.

v0:
```python
import jax
import jax.numpy as jnp
from jax import lax
from jax.sharding import PartitionSpec as P


def slot_tables(routing, route_gates, experts, capacity):
    count_rows = routing.shape[0]
    choices_n = routing.shape[1]
    flat_ids = routing.reshape(-1)
    onehot = (flat_ids[:, None] == jnp.arange(experts, dtype=jnp.int32)[None, :]).astype(jnp.int32)
    before = jnp.cumsum(onehot, axis=0) - onehot
    position = jnp.sum(before * onehot, axis=1)
    slot_index = flat_ids * capacity + position
    picked = (
        slot_index[:, None] == jnp.arange(experts * capacity, dtype=jnp.int32)[None, :]
    ).astype(jnp.float32)
    dispatch = picked.reshape(count_rows, choices_n, experts * capacity).sum(axis=1)
    combine = (
        (picked * route_gates.reshape(-1)[:, None])
        .reshape(count_rows, choices_n, experts * capacity)
        .sum(axis=1)
    )
    return (dispatch, combine)


def hidden_rows(everyone, expert_gate, expert_up, capacity):
    local_count = expert_gate.shape[0]
    total = everyone.shape[0]
    row_block = everyone.reshape(
        total // (local_count * capacity), local_count, capacity, everyone.shape[1]
    )
    gate_part = jnp.einsum(
        "tlcd,ldf->tlcf", row_block, expert_gate, preferred_element_type=jnp.float32
    )
    upward = jnp.einsum("tlcd,ldf->tlcf", row_block, expert_up, preferred_element_type=jnp.float32)
    return (jax.nn.silu(gate_part) * upward).astype(jnp.bfloat16)


def body(tokens, routing, route_gates, expert_gate, expert_up, expert_down):
    local_count = expert_gate.shape[0]
    ep_count = lax.axis_size("ep")
    tp_count = lax.axis_size("tp")
    tok_count = tokens.shape[0]
    capacity = 2 * tok_count // ep_count + tok_count // 16
    experts = local_count * ep_count
    dispatch, combine = slot_tables(routing, route_gates, experts, capacity)
    dispatch_low = dispatch.astype(jnp.bfloat16)
    whole = lax.all_gather(tokens, "tp", axis=1, tiled=True)
    packed = jnp.einsum(
        "tc,td->cd", dispatch_low, whole, preferred_element_type=jnp.float32
    ).astype(jnp.bfloat16)
    everyone = lax.all_to_all(packed, "ep", split_axis=0, concat_axis=0, tiled=True)
    total_rows = everyone.shape[0]
    columns = everyone.shape[1]
    hidden = hidden_rows(everyone, expert_gate, expert_up, capacity)
    part = jnp.einsum("tlcf,lfd->dtlc", hidden, expert_down, preferred_element_type=jnp.float32)
    summed_t = lax.psum_scatter(
        part.reshape(columns // tp_count * lax.axis_size("tp"), total_rows),
        "tp",
        scatter_dimension=0,
        tiled=True,
    )
    summed = summed_t.T
    expert_out = summed.astype(jnp.bfloat16)
    returned = lax.all_to_all(expert_out, "ep", split_axis=0, concat_axis=0, tiled=True)
    mixed = jnp.dot(combine, returned.astype(jnp.float32), precision=lax.Precision.HIGHEST)
    return mixed.astype(jnp.bfloat16)


def solution(mesh):
    return jax.shard_map(
        body,
        mesh=mesh,
        in_specs=(
            P(("rep", "ep"), "tp"),
            P(("rep", "ep"), None),
            P(("rep", "ep"), None),
            P("ep", None, "tp"),
            P("ep", None, "tp"),
            P("ep", "tp", None),
        ),
        out_specs=P(("rep", "ep"), "tp"),
        check_vma=False,
    )
```

profile of v0, /device:TPU:0, one launch (start us, length us, event | category | flops | bytes accessed | tf_op | source)
XLA Modules:
  0.0 145.9 jit_solution(12279673939200975978)
XLA Ops:
  6.5 0.0 reduce-scatter.2.cloned.1.call-start
  6.5 0.8 copy.23
  7.3 0.1 eq.37
  7.5 1.2 reduce-window.6
  8.7 0.1 slice.12
  8.8 0.1 copy.24
  8.9 0.1 copy.25
  9.0 0.1 add_bitcast_fusion
  9.1 0.1 reduce_sum.30
  9.3 0.1 copy.26
  9.3 0.7 multiply_add_fusion
  10.1 18.5 %all_gather.3 = bf16[96,3072]{1,0:T(8,128)(2,1)S(1)} all-gather(bf16[96,768]{1,0:T(8,128)(2,1)} %param.6), channel_id=1, replica_groups=mesh['rep'=2,'tp'=4,'ep'=4] {'tp'}, dimensions={1}, use_global_device_ids=true | all-gather | bytes 737280 | tf_op jit(solution)/shard_map/all_gather | solution.py:49
  28.5 0.8 convert_reduce_fusion
  29.3 0.5 convolution_convert_fusion
  29.9 0.4 all_to_all.14
  30.2 20.5 %all_to_all.21 = bf16[4,54,3072]{2,1,0:T(8,128)(2,1)S(1)} all-to-all(bf16[4,54,3072]{2,1,0:T(8,128)(2,1)S(1)} %all_to_all.14), channel_id=1, replica_groups=mesh['rep'=2,'tp'=4,'ep'=4] {'ep'}, dimensions={0} | all-to-all | bytes 2654208 | tf_op jit(solution)/shard_map/all_to_all | solution.py:53
  50.7 6.3 %fusion.9 = f32[4,1,54,2048]{3,2,0,1:T(8,128)S(1)} fusion(bf16[4,54,3072]{2,1,0:T(8,128)(2,1)S(1)} %all_to_all.21, bf16[1,3072,2048]{2,1,0:T(8,128)(2,1)} %param.9), kind=kOutput, calls=%fused_computation.8 | convolution fusion | flops 2717908992 | bytes 15679488 | tf_op jit(solution)/shard_map/tlcd,ldf->tlcf/dot_general | solution.py:33
  57.0 7.9 %fusion.18 = bf16[4,1,54,2048]{3,2,0,1:T(8,128)(2,1)S(1)} fusion(bf16[4,54,3072]{2,1,0:T(8,128)(2,1)S(1)} %all_to_all.21, bf16[1,3072,2048]{2,1,0:T(8,128)(2,1)} %param.10, f32[4,1,54,2048]{3,2,0,1:T(8,128)S(1)} %fusion.9), kind=kOutput, calls=%fused_computation.11 | convolution fusion | flops 2720563200 | bytes 16564224 | tf_op jit(solution)/shard_map/tlcd,ldf->tlcf/dot_general | solution.py:36
  64.9 0.2 dot_general.34
  65.1 9.0 %fusion.6 = f32[3072,216]{0,1:T(8,128)} fusion(bf16[216,2048]{1,0:T(8,128)(2,1)S(1)} %dot_general.34, bf16[1,2048,3072]{2,1,0:T(8,128)(2,1)} %param.11), kind=kOutput, calls=%fused_computation.6 | convolution fusion | flops 2717908992 | bytes 16121856 | tf_op jit(solution)/shard_map/tlcf,lfd->dtlc/dot_general | solution.py:57
  74.1 0.0 reduce-scatter.2.cloned.1.call-update
  74.2 53.2 %reduce-scatter.2.cloned.1.call-done = f32[768,216]{0,1:T(8,128)} async-done(((f32[3072,216]{0,1:T(8,128)}), f32[768,216]{0,1:T(8,128)}) %reduce-scatter.2.cloned.1.call-update) | async-done | bytes 663568 | tf_op jit(solution)/shard_map/reduce_scatter | solution.py:58
  127.4 1.1 convert_bitcast_fusion
  128.5 0.1 all_to_all.16
  128.6 9.4 %all_to_all.22 = bf16[4,54,768]{2,1,0:T(8,128)(2,1)S(1)} all-to-all(bf16[4,54,768]{2,1,0:T(8,128)(2,1)S(1)} %all_to_all.16), channel_id=1, replica_groups=mesh['rep'=2,'tp'=4,'ep'=4] {'ep'}, dimensions={0} | all-to-all | bytes 663552 | tf_op jit(solution)/shard_map/all_to_all | solution.py:66
  138.0 0.1 all_to_all.18
  138.1 1.0 convolution_convert_fusion.1
  (7 shorter events, 0.1 us)
Async XLA Ops:
  6.5 120.8 %reduce-scatter.2.cloned.1.call-start = ((), (), s32[]{:S(2)}) async-start(), calls=%async_computation.3 | async-start | bytes 3317760 | tf_op jit(solution)/shard_map/reduce_scatter | solution.py:58
Sparse Core Ops, SparseCore 0:
  74.3 53.0 reduce-scatter.1
where the time goes:
time: 146 us
  waiting for transfers between devices  53.2 us (36%)
  blocking collectives  48.4 us (33%)
  matrix products  24.6 us (17%)
  between operations  13.5 us (9%)
  other arithmetic  4.01 us (3%)
  local copies, waits for them, and re-layouts  2.2 us (2%)
    reduce_scatter x1, waiting for transfers between devices, body(): lax.psum_scatter(part.reshape(columns // tp_count * lax.axis_size('tp'),...  53.2 us
    all_to_all x1, blocking collectives, body(): lax.all_to_all(packed, 'ep', split_axis=0, concat_axis=0, tiled=True)  20.5 us
    all_gather x1, blocking collectives, body(): whole = lax.all_gather(tokens, 'tp', axis=1, tiled=True)  18.5 us
    all_to_all x1, blocking collectives, body(): lax.all_to_all(expert_out, 'ep', split_axis=0, concat_axis=0, tiled=True)  9.41 us
    dot_general x1, matrix products, body(): jnp.einsum('tlcf,lfd->dtlc', hidden, expert_down, preferred_element_type=...  9.01 us
    dot_general x1, matrix products, hidden_rows(): jnp.einsum('tlcd,ldf->tlcf', row_block, expert_up, preferred_element_type...  7.89 us
    dot_general x1, matrix products, hidden_rows(): jnp.einsum('tlcd,ldf->tlcf', row_block, expert_gate, preferred_element_ty...  6.26 us
  transfers between devices with their start and end apart: 1, of which 1 were waited for; matrix products, arithmetic and copies ran while one was open for 0% of the time, Pallas kernels for 0%

commit v1 on v0

--- a/solution.py
+++ b/solution.py
@@ -1,6 +1,10 @@
+import functools
+
 import jax
 import jax.numpy as jnp
 from jax import lax
+from jax.experimental import pallas as pl
+from jax.experimental.pallas import tpu as pltpu
 from jax.sharding import PartitionSpec as P
 
 
@@ -37,7 +41,7 @@
     return (jax.nn.silu(gate_part) * upward).astype(jnp.bfloat16)
 
 
-def body(tokens, routing, route_gates, expert_gate, expert_up, expert_down):
+def plain_body(tokens, routing, route_gates, expert_gate, expert_up, expert_down):
     local_count = expert_gate.shape[0]
     ep_count = lax.axis_size("ep")
     tp_count = lax.axis_size("tp")
@@ -68,6 +72,282 @@
     return mixed.astype(jnp.bfloat16)
 
 
+MESH = pl.DeviceIdType.MESH
+LANES = 128
+
+
+def up_to(value, step):
+    return -(-value // step) * step
+
+
+def rcopy(src, dst, send, recv, device):
+    return pltpu.make_async_remote_copy(
+        src_ref=src, dst_ref=dst, send_sem=send, recv_sem=recv, device_id=device, device_id_type=MESH
+    )
+
+
+def layer_kernel(
+    tp, ep, cap, rows, tokens, meta, gate_hbm, up_hbm, down_hbm, out,
+    x, m, pick, place, scale, wg, wu, wd, acc_g, acc_u, packed, hidden, part,
+    c, c_in, x_out, x_in, z_out, z_in,
+    w_sem, zs, zr, xs, xr, cs, cr, ms, mr, rcs, rcr, rxs, rxr, rzs, rzr,
+):
+    t = lax.axis_index("tp")
+    e = lax.axis_index("ep")
+    half = ep // 2
+    core = lax.rem(e, 2)
+    column = e // 2
+    e_core = e + 1 - 2 * core
+    e_x = lax.rem(e + half, ep)
+    e_xc = lax.rem(e_core + half, ep)
+    tok, feat = tokens.shape
+    ff = wg.shape[2]
+    f32, b16 = jnp.float32, jnp.bfloat16
+
+    def quarter(d):
+        return lax.rem(t + tp - d, tp)
+
+    loads = []
+    for d in range(tp):
+        q = quarter(d)
+        for k, (src, dst) in enumerate(((gate_hbm, wg), (up_hbm, wu))):
+            r = pl.ds(pl.multiple_of(q * feat, feat), feat)
+            loads.append(pltpu.make_async_copy(src.at[0, r, :], dst.at[q], w_sem.at[k * tp + d]))
+    down_loads = []
+    for i in range(tp):
+        q = quarter(tp - 1 - i)
+        r = pl.ds(pl.multiple_of(q * feat, feat), feat)
+        down_loads.append(pltpu.make_async_copy(down_hbm.at[0, :, r], wd.at[q], w_sem.at[2 * tp + i]))
+    for load in loads + down_loads:
+        load.start()
+
+    pad = x.shape[2] - tok
+    for q in range(tp):
+        for b in range(ep):
+            x[q, b, tok:, :] = jnp.zeros((pad, feat), b16)
+    x[t, e, 0:tok, :] = tokens[...]
+    m[e] = meta[...]
+    part[rows:, :] = jnp.zeros((part.shape[0] - rows, feat), b16)
+
+    barrier = pltpu.get_barrier_semaphore()
+    for d in range(1, tp):
+        pl.semaphore_signal(barrier, inc=1, device_id={"tp": lax.rem(t + d, tp)}, device_id_type=MESH)
+    pl.semaphore_signal(barrier, inc=1, device_id={"ep": e_x}, device_id_type=MESH)
+    pl.semaphore_signal(barrier, inc=1, device_id={"ep": e_core}, device_id_type=MESH)
+    pl.semaphore_wait(barrier, tp + 1)
+
+    sent = []
+
+    def send(src, dst, s, r, device):
+        copy = rcopy(src, dst, s, r, device)
+        copy.start()
+        sent.append(copy)
+
+    def block(q, b):
+        return x.at[q, b, pl.ds(0, tok), :]
+
+    to_x, to_core = {"ep": e_x}, {"ep": e_core}
+    send(meta, m.at[e], ms.at[0], mr.at[0], to_x)
+    send(meta, m.at[e], ms.at[1], mr.at[1], to_core)
+    send(tokens, block(t, e), xs.at[0], xr.at[0], to_x)
+    for d in range(1, tp):
+        send(tokens, block(t, e), zs.at[d], zr.at[d], {"tp": lax.rem(t + d, tp)})
+    send(tokens, block(t, e), cs.at[0], cr.at[0], to_core)
+
+    def got(dst, s, r, device):
+        rcopy(dst, dst, s, r, device).wait_recv()
+
+    def take_z(d):
+        q = quarter(d)
+        got(block(q, e), zs.at[d], zr.at[d], {"tp": q})
+        send(block(q, e), block(q, e), xs.at[d], xr.at[d], to_x)
+        send(block(q, e), block(q, e), cs.at[d], cr.at[d], to_core)
+
+    def take_x(d):
+        q = quarter(d)
+        got(block(q, e_x), xs.at[d], xr.at[d], to_x)
+        send(block(q, e_x), block(q, e_x), cs.at[tp + d], cr.at[tp + d], to_core)
+
+    def take_core(d):
+        q = quarter(d)
+        got(block(q, e_core), cs.at[d], cr.at[d], to_core)
+        got(block(q, e_xc), cs.at[tp + d], cr.at[tp + d], to_core)
+
+    got(m.at[e_x], ms.at[0], mr.at[0], to_x)
+    send(m.at[e_x], m.at[e_x], ms.at[2], mr.at[2], to_core)
+    got(m.at[e_core], ms.at[1], mr.at[1], to_core)
+    got(m.at[e_xc], ms.at[2], mr.at[2], to_core)
+
+    slots = pick.shape[0]
+    mine = e.astype(f32)
+    earlier = (
+        lax.broadcasted_iota(jnp.int32, (LANES, LANES), 0)
+        < lax.broadcasted_iota(jnp.int32, (LANES, LANES), 1)
+    ).astype(b16)
+    slot = lax.broadcasted_iota(jnp.int32, (slots, LANES), 0).astype(f32)
+    total = jnp.zeros((slots, 1), f32)
+    for b in range(ep):
+        first, second = m[b, 0:1, :] == mine, m[b, 1:2, :] == mine
+        named = jnp.where(first, 1.0, 0.0) + jnp.where(second, 1.0, 0.0)
+        weight = jnp.where(first, m[b, 2:3, :], 0.0) + jnp.where(second, m[b, 3:4, :], 0.0)
+        spread = jnp.broadcast_to(named, (16, LANES)).astype(b16)
+        position = jnp.dot(spread, earlier, preferred_element_type=f32)[0:1, :]
+        where_to = jnp.where(named > 0.5, position + float(b * cap), -1.0)
+        chosen = jnp.where(slot == where_to, 1.0, 0.0)
+        total = total + jnp.sum(chosen * weight, axis=1, keepdims=True)
+        pick[:, b * LANES:(b + 1) * LANES] = chosen.astype(b16)
+        at = ((b % 2) * half + b // 2) * tok
+        place[at:at + tok, :] = chosen.T[0:tok, :].astype(b16)
+    scale[...] = jnp.broadcast_to(total, scale.shape)
+
+    step = 512
+    tiles = ff // step
+
+    def project(d, last):
+        q = quarter(d)
+        loads[2 * d].wait()
+        loads[2 * d + 1].wait()
+        everyone = x[q].reshape(ep * x.shape[2], feat)
+        packed[...] = jnp.dot(pick[0:rows, :], everyone, preferred_element_type=f32).astype(b16)
+
+        def tile(j, carry):
+            cols = pl.ds(pl.multiple_of(j * step, step), step)
+            g = jnp.dot(packed[...], wg[q, :, cols], preferred_element_type=f32)
+            u = jnp.dot(packed[...], wu[q, :, cols], preferred_element_type=f32)
+            if d > 0:
+                g = g + acc_g[:, cols]
+                u = u + acc_u[:, cols]
+            if last:
+                h = g / (1.0 + jnp.exp(-g)) * u * scale[0:rows, 0:1]
+                hidden[:, cols] = h.astype(b16)
+            else:
+                acc_g[:, cols] = g
+                acc_u[:, cols] = u
+            return carry
+
+        lax.fori_loop(0, tiles, tile, 0)
+
+    take_x(0)
+    for d in range(1, tp):
+        take_z(d)
+        if d > 1:
+            take_x(d - 1)
+        take_core(d - 1)
+        project(d - 1, False)
+    take_x(tp - 1)
+    take_core(tp - 1)
+    project(tp - 1, True)
+
+    width = 256 if feat % 256 == 0 else LANES
+
+    def to_tokens(i):
+        q = quarter(tp - 1 - i)
+        down_loads[i].wait()
+
+        def tile(j, carry):
+            cols = pl.ds(pl.multiple_of(j * width, width), width)
+            part[0:rows, cols] = jnp.dot(hidden[...], wd[q, :, cols], preferred_element_type=f32).astype(b16)
+            back = jnp.dot(place[...], part[:, cols], preferred_element_type=f32).astype(b16)
+            c[i, :, :, cols] = back.reshape(ep, tok, width)
+            return carry
+
+        lax.fori_loop(0, feat // width, tile, 0)
+        away = pl.ds((1 - core) * half, half)
+        send(c.at[i, away], c_in.at[i], rcs.at[i], rcr.at[i], to_core)
+
+    def sum_core(i):
+        got(c_in.at[i], rcs.at[i], rcr.at[i], to_core)
+        far = 1 - column
+        value = c[i, core * half + far].astype(f32) + c_in[i, far].astype(f32)
+        x_out[i] = value.astype(b16)
+        send(x_out.at[i], x_in.at[i], rxs.at[i], rxr.at[i], to_x)
+
+    def sum_x(i):
+        got(x_in.at[i], rxs.at[i], rxr.at[i], to_x)
+        value = c[i, core * half + column].astype(f32) + c_in[i, column].astype(f32)
+        return value + x_in[i].astype(f32)
+
+    for i in range(tp):
+        to_tokens(i)
+        if i > 0:
+            sum_core(i - 1)
+    sum_core(tp - 1)
+    for i in range(tp - 1):
+        z_out[i] = sum_x(i).astype(b16)
+        send(z_out.at[i], z_in.at[i], rzs.at[i], rzr.at[i], {"tp": quarter(tp - 1 - i)})
+    result = sum_x(tp - 1)
+    for i in range(tp - 1):
+        got(z_in.at[i], rzs.at[i], rzr.at[i], {"tp": lax.rem(t + tp - 1 - i, tp)})
+        result = result + z_in[i].astype(f32)
+    out[...] = result.astype(b16)
+    for copy in sent:
+        copy.wait_send()
+
+
+def kernel_body(tokens, routing, route_gates, expert_gate, expert_up, expert_down):
+    ep, tp = lax.axis_size("ep"), lax.axis_size("tp")
+    tok, feat = tokens.shape
+    ff = expert_gate.shape[2]
+    cap = 2 * tok // ep + tok // 16
+    rows = up_to(ep * cap, 16)
+    slots = up_to(rows, LANES)
+    ids = jnp.pad(routing.astype(jnp.float32).T, ((0, 0), (0, LANES - tok)), constant_values=-1.0)
+    weights = jnp.pad(route_gates.T, ((0, 4), (0, LANES - tok)))
+    meta = jnp.concatenate([ids, weights], axis=0)
+    f32, b16 = jnp.float32, jnp.bfloat16
+    dma = pltpu.SemaphoreType.DMA
+    vmem = pl.BlockSpec(memory_space=pltpu.VMEM)
+    hbm = pl.BlockSpec(memory_space=pl.ANY)
+    return pl.pallas_call(
+        functools.partial(layer_kernel, tp, ep, cap, rows),
+        out_shape=jax.ShapeDtypeStruct((tok, feat), b16),
+        in_specs=[vmem, vmem, hbm, hbm, hbm],
+        out_specs=vmem,
+        scratch_shapes=[
+            pltpu.VMEM((tp, ep, LANES, feat), b16),
+            pltpu.VMEM((ep, 8, LANES), f32),
+            pltpu.VMEM((slots, ep * LANES), b16),
+            pltpu.VMEM((ep * tok, slots), b16),
+            pltpu.VMEM((slots, LANES), f32),
+            pltpu.VMEM((tp, feat, ff), b16),
+            pltpu.VMEM((tp, feat, ff), b16),
+            pltpu.VMEM((tp, ff, feat), b16),
+            pltpu.VMEM((rows, ff), f32),
+            pltpu.VMEM((rows, ff), f32),
+            pltpu.VMEM((rows, feat), b16),
+            pltpu.VMEM((rows, ff), b16),
+            pltpu.VMEM((slots, feat), b16),
+            pltpu.VMEM((tp, ep, tok, feat), b16),
+            pltpu.VMEM((tp, ep // 2, tok, feat), b16),
+            pltpu.VMEM((tp, tok, feat), b16),
+            pltpu.VMEM((tp, tok, feat), b16),
+            pltpu.VMEM((tp, tok, feat), b16),
+            pltpu.VMEM((tp, tok, feat), b16),
+            dma((3 * tp,)),
+            dma((tp,)), dma((tp,)),
+            dma((tp,)), dma((tp,)),
+            dma((2 * tp,)), dma((2 * tp,)),
+            dma((3,)), dma((3,)),
+            dma((tp,)), dma((tp,)),
+            dma((tp,)), dma((tp,)),
+            dma((tp,)), dma((tp,)),
+        ],
+        compiler_params=pltpu.CompilerParams(
+            collective_id=0, has_side_effects=True, vmem_limit_bytes=60 * 1024 * 1024
+        ),
+    )(tokens, meta, expert_gate, expert_up, expert_down)
+
+
+def body(tokens, routing, route_gates, expert_gate, expert_up, expert_down):
+    ep, tp = lax.axis_size("ep"), lax.axis_size("tp")
+    tok, feat = tokens.shape
+    ff = expert_gate.shape[2]
+    fits = ep == 4 and expert_gate.shape[0] == 1 and tok <= LANES and tok % 16 == 0
+    fits = fits and feat % LANES == 0 and ff % 512 == 0 and 3 * tp * feat * ff * 2 <= 40 << 20
+    run = kernel_body if fits else plain_body
+    return run(tokens, routing, route_gates, expert_gate, expert_up, expert_down)
+
+
 def solution(mesh):
     return jax.shard_map(
         body,

time: 146 us -> 60.5 us (0.41)
  Pallas kernels: 0 us -> 56 us
  waiting for transfers between devices: 53.2 us -> 0 us
  blocking collectives: 48.4 us -> 0 us
  matrix products: 24.6 us -> 0 us
  between operations: 13.5 us -> 0.01 us
  other arithmetic: 4.01 us -> 1.96 us
    pallas_call x0 -> x1, Pallas kernels: none -> 56 us  [kernel_body(): pl.pallas_call(functools.partial(layer_kernel, tp, ep, cap, rows), out_sh...]
    reduce_scatter x1 -> x0, waiting for transfers between devices: 53.2 us -> none  [body(): lax.psum_scatter(part.reshape(columns // tp_count * lax.axis_size('tp'),...]
    all_to_all x2 -> x0, blocking collectives: 29.9 us -> none  [the longest x1 20.5 us: body(): lax.all_to_all(packed, 'ep', split_axis=0, concat_axis=0, tiled=True)]
    dot_general x5 -> x0, matrix products: 24.6 us -> none  [the longest x1 9.01 us: body(): jnp.einsum('tlcf,lfd->dtlc', hidden, expert_down, preferred_element_type=...]
    all_gather x1 -> x0, blocking collectives: 18.5 us -> none  [body(): whole = lax.all_gather(tokens, 'tp', axis=1, tiled=True)]
  transfers between devices with their start and end apart: 1 -> 0, of which waited for: 1 -> 0; matrix products, arithmetic and copies ran while one was open for 0% -> 0% of each run, Pallas kernels for 0% -> 0%
where the time goes in v1:
time: 60.5 us; the launch traced here: 59.6 us
  Pallas kernels  56 us (93%)
  other arithmetic  1.96 us (3%)
  local copies, waits for them, and re-layouts  1.58 us (3%)
    pallas_call x1, Pallas kernels, kernel_body(): pl.pallas_call(functools.partial(layer_kernel, tp, ep, cap, rows), out_sh...  56 us
    unnamed x1, local copies, waits for them, and re-layouts  1.58 us
    concatenate x1, other arithmetic, kernel_body(): meta = jnp.concatenate([ids, weights], axis=0)  1.28 us

profile of v1, /device:TPU:0, one launch (start us, length us, event | category | flops | bytes accessed | tf_op | source)
XLA Modules:
  0.0 59.6 jit_solution(10376796663770392152)
XLA Ops:
  0.0 0.7 %convert_bitcast_fusion = f32[2,96]{1,0:T(2,128)S(1)} fusion(s32[96,2]{0,1:T(2,128)} %param.7), kind=kLoop, calls=%fused_computation.3 | loop fusion | flops 192 | bytes 1536 | tf_op jit(solution)/shard_map/transpose | solution.py:294
  0.7 1.3 %select_maximum_fusion.meta = f32[8,128]{1,0:T(8,128)} fusion(f32[2,96]{1,0:T(2,128)} %bitcast.3, f32[2,96]{1,0:T(2,128)S(1)} %convert_bitcast_fusion), kind=kLoop, calls=%fused_computation | loop fusion | flops 5120 | bytes 5632 | tf_op jit(solution)/shard_map/concatenate | solution.py:296
  2.0 56.0 %shard_map.64 = bf16[96,768]{1,0:T(8,128)(2,1)} custom-call(bf16[96,768]{1,0:T(8,128)(2,1)} %tokens.1, f32[8,128]{1,0:T(8,128)} %select_maximum_fusion.meta, bf16[1,3072,2048]{2,1,0:T(8,128)(2,1)} %gate_hbm.1, bf16[1,3072,2048]{2,1,0:T(8,128)(2,1)} %up_hbm.1, bf16[1,2048,3072]{2,1,0:T(8,128)(2,1)} %down_hbm.1), custom_call_target="tpu_custom_call" | custom-call | tf_op jit(solution)/shard_map/pallas_call | solution.py:301
  58.0 1.6 %copy.8 = bf16[96,768]{1,0:T(8,128)(2,1)} copy(bf16[96,768]{1,0:T(8,128)(2,1)} %shard_map.64) | data formatting | bytes 294912

commit v2 on v1

--- a/solution.py
+++ b/solution.py
@@ -107,9 +107,20 @@
     def quarter(d):
         return lax.rem(t + tp - d, tp)
 
+    def select(values):
+        found = jnp.int32(values[0])
+        for k in range(1, tp):
+            found = jnp.where(t == k, jnp.int32(values[k]), found)
+        return found
+
+    nearest = [sorted(range(tp), key=lambda q, k=k: (abs(q - k), q)) for k in range(tp)]
+    arrivals = [select([nearest[k][i] for k in range(tp)]) for i in range(tp)]
+    pieces = 2 if tok % 32 == 0 else 1
+    piece = tok // pieces
+
     loads = []
     for d in range(tp):
-        q = quarter(d)
+        q = arrivals[d]
         for k, (src, dst) in enumerate(((gate_hbm, wg), (up_hbm, wu))):
             r = pl.ds(pl.multiple_of(q * feat, feat), feat)
             loads.append(pltpu.make_async_copy(src.at[0, r, :], dst.at[q], w_sem.at[k * tp + d]))
@@ -143,35 +154,59 @@
         copy.start()
         sent.append(copy)
 
-    def block(q, b):
-        return x.at[q, b, pl.ds(0, tok), :]
+    def block(q, b, p):
+        return x.at[q, b, pl.ds(p * piece, piece), :]
+
+    some = []
+
+    def send_if(cond, src, dst, s, r, device):
+        copy = rcopy(src, dst, s, r, device)
+        some.append((cond, copy))
+
+        @pl.when(cond)
+        def _():
+            copy.start()
 
     to_x, to_core = {"ep": e_x}, {"ep": e_core}
     send(meta, m.at[e], ms.at[0], mr.at[0], to_x)
     send(meta, m.at[e], ms.at[1], mr.at[1], to_core)
-    send(tokens, block(t, e), xs.at[0], xr.at[0], to_x)
-    for d in range(1, tp):
-        send(tokens, block(t, e), zs.at[d], zr.at[d], {"tp": lax.rem(t + d, tp)})
-    send(tokens, block(t, e), cs.at[0], cr.at[0], to_core)
+    above, below = {"tp": lax.rem(t + 1, tp)}, {"tp": lax.rem(t + tp - 1, tp)}
+    for p in range(pieces):
+        own = tokens.at[pl.ds(p * piece, piece), :]
+        n = pieces * t + p
+        send_if(t < tp - 1, own, block(t, e, p), zs.at[n], zr.at[n], above)
+        send_if(t > 0, own, block(t, e, p), zs.at[pieces * tp + n], zr.at[n], below)
+        send(own, block(t, e, p), xs.at[n], xr.at[n], to_x)
+        send(own, block(t, e, p), cs.at[n], cr.at[n], to_core)
 
     def got(dst, s, r, device):
         rcopy(dst, dst, s, r, device).wait_recv()
 
-    def take_z(d):
-        q = quarter(d)
-        got(block(q, e), zs.at[d], zr.at[d], {"tp": q})
-        send(block(q, e), block(q, e), xs.at[d], xr.at[d], to_x)
-        send(block(q, e), block(q, e), cs.at[d], cr.at[d], to_core)
-
-    def take_x(d):
-        q = quarter(d)
-        got(block(q, e_x), xs.at[d], xr.at[d], to_x)
-        send(block(q, e_x), block(q, e_x), cs.at[tp + d], cr.at[tp + d], to_core)
-
-    def take_core(d):
-        q = quarter(d)
-        got(block(q, e_core), cs.at[d], cr.at[d], to_core)
-        got(block(q, e_xc), cs.at[tp + d], cr.at[tp + d], to_core)
+    def take_z(i):
+        q = arrivals[i]
+        for p in range(pieces):
+            n = pieces * q + p
+            one = block(q, e, p)
+            got(one, zs.at[n], zr.at[n], above)
+            send_if((q < t) & (t < tp - 1), one, one, zs.at[n], zr.at[n], above)
+            send_if((q > t) & (t > 0), one, one, zs.at[pieces * tp + n], zr.at[n], below)
+            send(one, one, xs.at[n], xr.at[n], to_x)
+            send(one, one, cs.at[n], cr.at[n], to_core)
+
+    def take_x(i):
+        for p in range(pieces):
+            n = pieces * arrivals[i] + p
+            far = pieces * tp + n
+            one = block(arrivals[i], e_x, p)
+            got(one, xs.at[n], xr.at[n], to_x)
+            send(one, one, cs.at[far], cr.at[far], to_core)
+
+    def take_core(i):
+        for p in range(pieces):
+            n = pieces * arrivals[i] + p
+            far = pieces * tp + n
+            got(block(arrivals[i], e_core, p), cs.at[n], cr.at[n], to_core)
+            got(block(arrivals[i], e_xc, p), cs.at[far], cr.at[far], to_core)
 
     got(m.at[e_x], ms.at[0], mr.at[0], to_x)
     send(m.at[e_x], m.at[e_x], ms.at[2], mr.at[2], to_core)
@@ -204,7 +239,7 @@
     tiles = ff // step
 
     def project(d, last):
-        q = quarter(d)
+        q = arrivals[d]
         loads[2 * d].wait()
         loads[2 * d + 1].wait()
         everyone = x[q].reshape(ep * x.shape[2], feat)
@@ -228,15 +263,18 @@
         lax.fori_loop(0, tiles, tile, 0)
 
     take_x(0)
-    for d in range(1, tp):
-        take_z(d)
-        if d > 1:
-            take_x(d - 1)
-        take_core(d - 1)
-        project(d - 1, False)
-    take_x(tp - 1)
-    take_core(tp - 1)
-    project(tp - 1, True)
+    for i in range(1, tp - 1):
+        take_z(i)
+    if tp > 2:
+        take_x(1)
+    take_core(0)
+    project(0, tp == 1)
+    take_z(tp - 1)
+    for i in range(1, tp):
+        if i + 1 < tp:
+            take_x(i + 1)
+        take_core(i)
+        project(i, i == tp - 1)
 
     width = 256 if feat % 256 == 0 else LANES
 
@@ -255,17 +293,25 @@
         away = pl.ds((1 - core) * half, half)
         send(c.at[i, away], c_in.at[i], rcs.at[i], rcr.at[i], to_core)
 
+    def part_of(p):
+        return slice(p * piece, (p + 1) * piece)
+
     def sum_core(i):
         got(c_in.at[i], rcs.at[i], rcr.at[i], to_core)
         far = 1 - column
-        value = c[i, core * half + far].astype(f32) + c_in[i, far].astype(f32)
-        x_out[i] = value.astype(b16)
-        send(x_out.at[i], x_in.at[i], rxs.at[i], rxr.at[i], to_x)
-
-    def sum_x(i):
-        got(x_in.at[i], rxs.at[i], rxr.at[i], to_x)
-        value = c[i, core * half + column].astype(f32) + c_in[i, column].astype(f32)
-        return value + x_in[i].astype(f32)
+        for p in range(pieces):
+            r = part_of(p)
+            value = c[i, core * half + far, r].astype(f32) + c_in[i, far, r].astype(f32)
+            x_out[i, r] = value.astype(b16)
+            n = pieces * i + p
+            view = pl.ds(p * piece, piece)
+            send(x_out.at[i, view], x_in.at[i, view], rxs.at[n], rxr.at[n], to_x)
+
+    def sum_x(i, p):
+        r, n = part_of(p), pieces * i + p
+        got(x_in.at[i, pl.ds(p * piece, piece)], rxs.at[n], rxr.at[n], to_x)
+        value = c[i, core * half + column, r].astype(f32) + c_in[i, column, r].astype(f32)
+        return value + x_in[i, r].astype(f32)
 
     for i in range(tp):
         to_tokens(i)
@@ -273,13 +319,26 @@
             sum_core(i - 1)
     sum_core(tp - 1)
     for i in range(tp - 1):
-        z_out[i] = sum_x(i).astype(b16)
-        send(z_out.at[i], z_in.at[i], rzs.at[i], rzr.at[i], {"tp": quarter(tp - 1 - i)})
-    result = sum_x(tp - 1)
-    for i in range(tp - 1):
-        got(z_in.at[i], rzs.at[i], rzr.at[i], {"tp": lax.rem(t + tp - 1 - i, tp)})
-        result = result + z_in[i].astype(f32)
-    out[...] = result.astype(b16)
+        for p in range(pieces):
+            z_out[i, part_of(p)] = sum_x(i, p).astype(b16)
+            n = pieces * i + p
+            view = pl.ds(p * piece, piece)
+            peer = {"tp": quarter(tp - 1 - i)}
+            send(z_out.at[i, view], z_in.at[i, view], rzs.at[n], rzr.at[n], peer)
+    for p in range(pieces):
+        result = sum_x(tp - 1, p)
+        for i in range(tp - 1):
+            n = pieces * i + p
+            peer = {"tp": lax.rem(t + tp - 1 - i, tp)}
+            got(z_in.at[i, pl.ds(p * piece, piece)], rzs.at[n], rzr.at[n], peer)
+            result = result + z_in[i, part_of(p)].astype(f32)
+        out[part_of(p), :] = result.astype(b16)
+    for cond, copy in some:
+
+        @pl.when(cond)
+        def _(copy=copy):
+            copy.wait_send()
+
     for copy in sent:
         copy.wait_send()
 
@@ -324,13 +383,13 @@
             pltpu.VMEM((tp, tok, feat), b16),
             pltpu.VMEM((tp, tok, feat), b16),
             dma((3 * tp,)),
-            dma((tp,)), dma((tp,)),
+            dma((4 * tp,)), dma((2 * tp,)),
+            dma((2 * tp,)), dma((2 * tp,)),
+            dma((4 * tp,)), dma((4 * tp,)),
+            dma((3,)), dma((3,)),
             dma((tp,)), dma((tp,)),
             dma((2 * tp,)), dma((2 * tp,)),
-            dma((3,)), dma((3,)),
-            dma((tp,)), dma((tp,)),
-            dma((tp,)), dma((tp,)),
-            dma((tp,)), dma((tp,)),
+            dma((2 * tp,)), dma((2 * tp,)),
         ],
         compiler_params=pltpu.CompilerParams(
             collective_id=0, has_side_effects=True, vmem_limit_bytes=60 * 1024 * 1024
@@ -342,7 +401,7 @@
     ep, tp = lax.axis_size("ep"), lax.axis_size("tp")
     tok, feat = tokens.shape
     ff = expert_gate.shape[2]
-    fits = ep == 4 and expert_gate.shape[0] == 1 and tok <= LANES and tok % 16 == 0
+    fits = ep == 4 and tp > 2 and expert_gate.shape[0] == 1 and tok <= LANES and tok % 16 == 0
     fits = fits and feat % LANES == 0 and ff % 512 == 0 and 3 * tp * feat * ff * 2 <= 40 << 20
     run = kernel_body if fits else plain_body
     return run(tokens, routing, route_gates, expert_gate, expert_up, expert_down)

time: 60.5 us -> 56.7 us (0.937); the launches traced: 59.6 us -> 56.5 us
  Pallas kernels: 56 us -> 52.9 us
    pallas_call x1, Pallas kernels: 56 us -> 52.9 us  [kernel_body(): pl.pallas_call(functools.partial(layer_kernel, tp, ep, cap, rows), out_sh...]
where the time goes in v2:
time: 56.7 us; the launch traced here: 56.5 us
  Pallas kernels  52.9 us (93%)
  other arithmetic  1.96 us (3%)
  local copies, waits for them, and re-layouts  1.58 us (3%)
    pallas_call x1, Pallas kernels, kernel_body(): pl.pallas_call(functools.partial(layer_kernel, tp, ep, cap, rows), out_sh...  52.9 us
    unnamed x1, local copies, waits for them, and re-layouts  1.58 us
    concatenate x1, other arithmetic, kernel_body(): meta = jnp.concatenate([ids, weights], axis=0)  1.28 us

profile of v2, /device:TPU:0, one launch (start us, length us, event | category | flops | bytes accessed | tf_op | source)
XLA Modules:
  0.0 56.5 jit_solution(8677646399630796606)
XLA Ops:
  0.0 0.7 %convert_bitcast_fusion = f32[2,96]{1,0:T(2,128)S(1)} fusion(s32[96,2]{0,1:T(2,128)} %param.7), kind=kLoop, calls=%fused_computation.3 | loop fusion | flops 192 | bytes 1536 | tf_op jit(solution)/shard_map/transpose | solution.py:353
  0.7 1.3 %select_maximum_fusion.meta = f32[8,128]{1,0:T(8,128)} fusion(f32[2,96]{1,0:T(2,128)} %bitcast.3, f32[2,96]{1,0:T(2,128)S(1)} %convert_bitcast_fusion), kind=kLoop, calls=%fused_computation | loop fusion | flops 5120 | bytes 5632 | tf_op jit(solution)/shard_map/concatenate | solution.py:355
  2.0 52.9 %shard_map.64 = bf16[96,768]{1,0:T(8,128)(2,1)} custom-call(bf16[96,768]{1,0:T(8,128)(2,1)} %tokens.1, f32[8,128]{1,0:T(8,128)} %select_maximum_fusion.meta, bf16[1,3072,2048]{2,1,0:T(8,128)(2,1)} %gate_hbm.1, bf16[1,3072,2048]{2,1,0:T(8,128)(2,1)} %up_hbm.1, bf16[1,2048,3072]{2,1,0:T(8,128)(2,1)} %down_hbm.1), custom_call_target="tpu_custom_call" | custom-call | tf_op jit(solution)/shard_map/pallas_call | solution.py:360
  54.9 1.6 %copy.8 = bf16[96,768]{1,0:T(8,128)(2,1)} copy(bf16[96,768]{1,0:T(8,128)(2,1)} %shard_map.64) | data formatting | bytes 294912
